TPU v7x, 128 devices: a whole 4x4x4 slice. The times are simulated.
128 devices in a mesh: slab: 32 (over y, x, core), site: 4 (over z).
Axes of the slice: x: 4, y: 4, z: 4, core: 2. Of those that a mesh axis runs over, the one named last changes fastest.
Arguments:
- potential: float32 [3, 256, 256, 256], P(None, 'slab', 'site'), may hold values from -12 to 12
- t_now: float32 [3, 256, 256, 256], P(None, 'slab', 'site'), may hold values from -3 to 3
- hist_t: float32 [4, 3, 256, 256, 256], P(None, None, 'slab', 'site'), may hold values from -3 to 3
- hist_r: float32 [4, 3, 256, 256, 256], P(None, None, 'slab', 'site'), may hold values from -15 to 15
- chi_self: float32 [3, 256, 256, 256], P(None, ('slab', 'site')), may hold values from 0.3 to 3, as said below
- chi_cross: float32 [3, 256, 256, 256], P(None, ('slab', 'site')), may hold values from -1.8 to 1.8, as said below
Outputs:
- t_next: float32 [3, 256, 256, 256], P(None, 'slab', 'site')
- residual_last: float32 [3, 256, 256, 256], P(None, 'slab', 'site')
Inputs may be any that keep to these rules, and one draw needn't show every extreme that they name: `chi_self`: even in the wave vector: the entry at (kx, ky, kz) equals that at (-kx, -ky, -kz), indices taken modulo the grid. `chi_cross`: even in the wave vector: the entry at (kx, ky, kz) equals that at (-kx, -ky, -kz), indices taken modulo the grid.
All inputs are finite; a program needn't handle non-finite values.
Results may differ from a plain program's by a relative error of at most 0.0003.
Values sent between devices are 32-bit elements; how exact they have to be, the bound alone decides.
A program may use at most 192 MiB of HBM per device.

v0:
```python
import functools
import math

import jax
import jax.numpy as jnp
import numpy as np
from jax import lax
from jax.experimental import pallas as pl
from jax.experimental.pallas import tpu as pltpu
from jax.sharding import PartitionSpec as P

N = 256
HALF = N // 2
SITES = 3
HIST = 4
MIXING = 0.5
MESH = pl.DeviceIdType.MESH
F32 = jnp.float32
BF16 = jnp.bfloat16

ROWS = 512
PEERS = 127

NT = (((1,), (1,)), ((), ()))
NN = (((1,), (0,)), ((), ()))


def split_table(table):
    high = table.astype(np.float32).astype(jnp.bfloat16)
    low = (table - high.astype(np.float64)).astype(np.float32).astype(jnp.bfloat16)
    return np.stack([high, low])


def tables():
    index = np.arange(N)
    angles = (index[:, None] * index[None, :] % N) * (2.0 * math.pi / N)
    cosine, sine = np.cos(angles), np.sin(angles)
    imag_rows = -sine[:HALF].copy()
    imag_rows[0] = 1.0 - 2.0 * (index % 2)
    along_z = np.concatenate([cosine[:HALF], imag_rows], 0)
    along_x = np.concatenate([cosine, sine], 0)
    blocks = np.stack([cosine.reshape(N, 4, 64), sine.reshape(N, 4, 64)], 2).reshape(N, 512)
    turned = np.stack([-sine.reshape(N, 4, 64), cosine.reshape(N, 4, 64)], 2).reshape(N, 512)
    along_y = np.concatenate([blocks, turned], 0)
    return split_table(along_z), split_table(along_x), split_table(along_y)


def halves(value):
    high = value.astype(BF16)
    low = (value - high.astype(F32)).astype(BF16)
    return high, low


def solve_weights(gram):
    count = HIST + 1
    factor = [[None] * count for member in range(count)]
    for column in range(count):
        diagonal_sum = gram[column][column]
        for inner in range(column):
            diagonal_sum = diagonal_sum - factor[column][inner] * factor[column][inner]
        factor[column][column] = jnp.sqrt(diagonal_sum)
        for row in range(column + 1, count):
            entry = gram[row][column]
            for inner in range(column):
                entry = entry - factor[row][inner] * factor[column][inner]
            factor[row][column] = entry / factor[column][column]
    middle = []
    for row in range(count):
        entry = jnp.ones_like(gram[0][0])
        for inner in range(row):
            entry = entry - factor[row][inner] * middle[inner]
        middle.append(entry / factor[row][row])
    weights = [None] * count
    for row in range(count - 1, -1, -1):
        entry = middle[row]
        for inner in range(row + 1, count):
            entry = entry - factor[inner][row] * weights[inner]
        weights[row] = entry / factor[row][row]
    total = weights[0]
    for row in range(1, count):
        total = total + weights[row]
    return [weight / total for weight in weights]


PAIRS = [(i, j) for i in range(HIST) for j in range(i, HIST)]


def kernel(
    pot_hbm, t_hbm, hist_t_hbm, hist_r_hbm, self_hbm, cross_hbm, wz_hbm, cs_hbm, h_hbm,
    next_hbm, last_hbm,
    tv, hv, ut, hr, low_chi, top_chi,
    wz_wide, wz_tall, cs_wide, h_wide, h_tall,
    sent, got, spec, spec_top, back, home,
    d_b, z_f, r_b, zz_f, u_b, m_b, t_b, e_b, y_f,
    g_row, g_one, g_mid, g_two, res,
    in_sem, out_sem, fsend, frecv, bsend, brecv, gsend, grecv,
):
    slab = lax.axis_index("slab")
    site = lax.axis_index("site")
    plane = slab // 2
    py, px, core = plane // 4, plane % 4, slab % 2
    me = slab * 4 + site
    leading = me == 0

    counter = [0]
    copies = {}

    def load(name, src, dst):
        copy = pltpu.make_async_copy(src, dst, in_sem.at[counter[0]])
        counter[0] += 1
        copies[name] = copy
        copy.start()

    for q in range(SITES):
        load(("t", q), t_hbm.at[q], tv.at[q])
        load(("p", q), pot_hbm.at[q], hv.at[q])
        if q == 0:
            load("wz0", wz_hbm.at[0], wz_wide.at[:, pl.ds(0, 256)])
            load("wz1", wz_hbm.at[1], wz_wide.at[:, pl.ds(256, 256)])
            load("wz2", wz_hbm.at[0], wz_wide.at[:, pl.ds(512, 256)])
    load("r", hist_r_hbm, hr)
    load("u", hist_t_hbm, ut)
    for part in range(3):
        load(("cs", part), cs_hbm.at[part % 2], cs_wide.at[:, pl.ds(256 * part, 256)])
        load(("hw", part), h_hbm.at[part % 2], h_wide.at[:, pl.ds(512 * part, 512)])
    for a in range(SITES):
        load(("sl", a), self_hbm.at[a, 0], low_chi.at[a])
        load(("cl", a), cross_hbm.at[a, 0], low_chi.at[3 + a])
        load(("st", a), self_hbm.at[a, 1], top_chi.at[a])
        load(("ct", a), cross_hbm.at[a, 1], top_chi.at[3 + a])
    for part in range(3):
        load(("ht", part), h_hbm.at[part % 2], h_tall.at[pl.ds(512 * part, 512)])
        load(("wt", part), wz_hbm.at[part % 2], wz_tall.at[pl.ds(256 * part, 256)])

    cores = [core, (core + 1) % 2]
    zs = [(site + step) % 4 for step in range(4)]

    def chip(group):
        return ((py + group // 4) % 4) * 4 + (px + group % 4) % 4

    def over_peers(action):
        base = chip(0) * 2
        for near in range(1, 8):
            action(base + cores[near // 4], zs[near % 4])

        def step(group, carry):
            base = chip(group) * 2
            for near in range(8):
                action(base + cores[near // 4], zs[near % 4])
            return carry

        lax.fori_loop(1, 16, step, 0)

    barrier = pltpu.get_barrier_semaphore()
    over_peers(
        lambda sl, st: pl.semaphore_signal(
            barrier, inc=1, device_id=(sl, st), device_id_type=MESH
        )
    )

    lane = lax.broadcasted_iota(jnp.int32, (1, 128), 1)
    real_half = lane < 64

    def swap(value):
        return pltpu.roll(value, 64, 1)

    def forward_site(q):
        def chunk(c, carry):
            rows = pl.ds(pl.multiple_of(c * 64, 64), 64)
            indirect = tv[q, rows, :]
            field = indirect - hv[q, rows, :]
            total = jnp.where(field > 0, field, jnp.exp(jnp.minimum(field, 0.0)) - 1.0)
            hv[q, rows, :] = total
            high, low = halves(total - indirect)
            d_b[rows, 0:256] = high
            d_b[rows, 256:512] = high
            d_b[rows, 512:768] = low
            return carry

        lax.fori_loop(0, ROWS // 64, chunk, 0)
        z_f[...] = lax.dot_general(wz_wide[...], d_b[...], NT, preferred_element_type=F32)
        for pair in range(4):
            columns = pl.ds(128 * pair, 128)
            real, imag = z_f[0:128, columns], z_f[128:256, columns]
            first = jnp.where(real_half, real, swap(imag))
            second = jnp.where(real_half, swap(real), imag)
            sent[q, pl.ds(2 * pair, 128, stride=8), :] = first
            sent[q, pl.ds(2 * pair + 1, 128, stride=8), :] = second

    def send_forward(q):
        def action(sl, st):
            wave = pl.multiple_of((sl * 4 + st) * 8, 8)
            pltpu.make_async_remote_copy(
                src_ref=sent.at[q, pl.ds(wave, 8)],
                dst_ref=got.at[q, site, pl.ds(pl.multiple_of(slab * 8, 8), 8)],
                send_sem=fsend.at[q],
                recv_sem=frecv.at[q],
                device_id=(sl, st),
                device_id_type=MESH,
            ).start()

        over_peers(action)
        got[q, site, pl.ds(pl.multiple_of(slab * 8, 8), 8), :] = sent[
            q, pl.ds(pl.multiple_of(me * 8, 8), 8), :
        ]

    for q in range(SITES):
        copies[("t", q)].wait()
        copies[("p", q)].wait()
        if q == 0:
            for part in range(3):
                copies[f"wz{part}"].wait()
        forward_site(q)
        if q == 0:
            pl.semaphore_wait(barrier, PEERS)
        send_forward(q)

    copies["r"].wait()
    copies["u"].wait()

    def history(c, sums):
        rows = pl.ds(pl.multiple_of(c * 8, 8), 8)
        rs = [hr[i, rows, :] for i in range(HIST)]
        for i in range(HIST):
            ut[i, rows, :] = ut[i, rows, :] + MIXING * rs[i]
        return tuple(s + rs[i] * rs[j] for s, (i, j) in zip(sums, PAIRS))

    zero = jnp.zeros((8, 256), F32)
    past = lax.fori_loop(0, SITES * ROWS // 8, history, (zero,) * len(PAIRS))
    for part in range(3):
        copies[("cs", part)].wait()
        copies[("hw", part)].wait()
        copies[("ht", part)].wait()
        copies[("wt", part)].wait()
    for a in range(SITES):
        for kind in ("sl", "cl", "st", "ct"):
            copies[(kind, a)].wait()

    def arrived(sem):
        block = sent.at[0, pl.ds(0, PEERS * 8)]
        pltpu.make_async_copy(block, block, sem).wait()

    def along_y(pick, target, q):
        for s in range(4):
            columns = pl.ds(128 * s, 128)
            one, two = zz_f[0:256, columns], zz_f[256:512, columns]
            high, low = halves(pick(one, two))
            u_b[:, pl.ds(128 * s, 128)] = high
            u_b[:, pl.ds(512 + 128 * s, 128)] = high
            u_b[:, pl.ds(1024 + 128 * s, 128)] = low
        target[q] = lax.dot_general(h_wide[...], u_b[...], NT, preferred_element_type=F32)

    def pick_whole(one, two):
        other = swap(two)
        return one + jnp.where(real_half, other, -other)

    def pick_low(one, two):
        return jnp.where(real_half, one, -swap(two))

    def pick_top(one, two):
        return jnp.where(real_half, swap(one), -two)

    def plane_site(q, carry):
        arrived(frecv.at[q])
        for s in range(4):
            columns = pl.ds(128 * s, 128)
            high, low = halves(got[q, s])
            r_b[0:256, columns] = high
            r_b[256:512, columns] = high
            r_b[512:768, columns] = low
        zz_f[...] = lax.dot_general(cs_wide[...], r_b[...], NN, preferred_element_type=F32)

        @pl.when(leading)
        def _():
            along_y(pick_low, spec, q)
            along_y(pick_top, spec_top, q)

        @pl.when(jnp.logical_not(leading))
        def _():
            along_y(pick_whole, spec, q)

        return carry

    lax.fori_loop(0, SITES, plane_site, 0)

    def combine(chi, field, a, rows, upper):
        total = None
        for g in range(SITES):
            entry = chi[jnp.where(a == g, a, a + g + 2), rows, :]
            term = entry * field[g, upper, :]
            total = term if total is None else total + term
        return total

    def store_mixed(rows, value):
        high, low = halves(value)
        m_b[rows, 0:256] = high
        m_b[rows, 256:512] = high
        m_b[rows, 512:768] = low

    def back_site(a, carry):
        def mix(c, carry):
            rows = pl.ds(pl.multiple_of(c * 32, 32), 32)
            lower = pl.ds(pl.multiple_of(256 + c * 32, 32), 32)
            real = combine(low_chi, spec, a, rows, rows)
            imag = combine(low_chi, spec, a, rows, lower)

            @pl.when(leading)
            def _():
                top_real = combine(top_chi, spec_top, a, rows, rows)
                top_imag = combine(top_chi, spec_top, a, rows, lower)
                store_mixed(rows, (real - top_imag) * (1.0 / N**3))
                store_mixed(lower, (imag + top_real) * (1.0 / N**3))

            @pl.when(jnp.logical_not(leading))
            def _():
                store_mixed(rows, real * (2.0 / N**3))
                store_mixed(lower, imag * (2.0 / N**3))

            return carry

        lax.fori_loop(0, 8, mix, 0)
        zz_f[...] = lax.dot_general(cs_wide[...], m_b[...], NT, preferred_element_type=F32)
        for block in range(4):
            rows, lower = pl.ds(64 * block, 64), pl.ds(256 + 64 * block, 64)
            real = zz_f[rows, 0:256] - zz_f[lower, 256:512]
            imag = zz_f[rows, 256:512] + zz_f[lower, 0:256]
            for place, value in ((0, real), (256, imag)):
                high, low = halves(value)
                t_b[rows, pl.ds(place, 256)] = high
                t_b[rows, pl.ds(512 + place, 256)] = high
                t_b[rows, pl.ds(1024 + place, 256)] = low
        planes = lax.dot_general(t_b[...], h_tall[...], NN, preferred_element_type=F32)
        for s in range(4):
            back[a, s] = planes[:, 128 * s : 128 * s + 128]

        def action(sl, st):
            pltpu.make_async_remote_copy(
                src_ref=back.at[a, st, pl.ds(pl.multiple_of(sl * 8, 8), 8)],
                dst_ref=home.at[a, pl.ds(pl.multiple_of(me * 8, 8), 8)],
                send_sem=bsend.at[a],
                recv_sem=brecv.at[a],
                device_id=(sl, st),
                device_id_type=MESH,
            ).start()

        over_peers(action)
        home[a, pl.ds(pl.multiple_of(me * 8, 8), 8), :] = back[
            a, site, pl.ds(pl.multiple_of(slab * 8, 8), 8), :
        ]
        return carry

    lax.fori_loop(0, SITES, back_site, 0)

    def home_site(a, sums):
        arrived(brecv.at[a])
        for x in range(8):
            lines = jnp.transpose(home[a, pl.ds(x, 128, stride=8), :])
            high, low = halves(jnp.concatenate([lines[0:64], lines[64:128]], 1))
            rows = pl.ds(64 * x, 64)
            e_b[rows, 0:256] = high
            e_b[rows, 256:512] = high
            e_b[rows, 512:768] = low
        y_f[...] = lax.dot_general(e_b[...], wz_tall[...], NN, preferred_element_type=F32)

        def chunk(c, sums):
            rows = pl.ds(pl.multiple_of(c * 8, 8), 8)
            latest = y_f[rows, :] - hv[a, rows, :]
            hv[a, rows, :] = latest
            tv[a, rows, :] = tv[a, rows, :] + MIXING * latest
            offset = pl.ds(pl.multiple_of(a * ROWS + c * 8, 8), 8)
            new = [s + hr[i, offset, :] * latest for i, s in enumerate(sums[:HIST])]
            return tuple(new) + (sums[HIST] + latest * latest,)

        sums = lax.fori_loop(0, ROWS // 8, chunk, sums)
        pltpu.make_async_copy(hv.at[a], last_hbm.at[a], out_sem.at[a]).start()
        return sums

    newest = lax.fori_loop(0, SITES, home_site, (zero,) * (HIST + 1))

    entries = {pair: s for pair, s in zip(PAIRS, past)}
    for i in range(HIST + 1):
        entries[(i, HIST)] = newest[i]
    order = sorted(entries)
    row = jnp.zeros((1, 128), F32)
    for place, pair in enumerate(order):
        folded = entries[pair][:, 0:128] + entries[pair][:, 128:256]
        value = jnp.sum(jnp.sum(folded, axis=0, keepdims=True), axis=1, keepdims=True)
        row = jnp.where(lane == place, value, row)
    g_row[0:1, :] = row

    def send_row(src, dst, slot, stage, sl, st):
        pltpu.make_async_remote_copy(
            src_ref=src.at[pl.ds(0, 1)],
            dst_ref=dst.at[pl.ds(slot, 1)],
            send_sem=gsend.at[stage],
            recv_sem=grecv.at[stage],
            device_id=(sl, st),
            device_id_type=MESH,
        ).start()

    for near in range(1, 2):
        send_row(g_row, g_one, slab, 0, chip(0) * 2 + cores[near], site)

    def spread(group, carry):
        for near in range(2):
            send_row(g_row, g_one, slab, 0, chip(group) * 2 + cores[near], site)
        return carry

    lax.fori_loop(1, 16, spread, 0)
    g_one[pl.ds(slab, 1), :] = row

    def wait_rows(count, sem):
        block = g_one.at[pl.ds(0, count)]
        pltpu.make_async_copy(block, block, sem).wait()

    wait_rows(31, grecv.at[0])
    partial = jnp.sum(g_one[...], axis=0, keepdims=True)
    g_mid[0:1, :] = partial
    for near in range(1, 4):
        send_row(g_mid, g_two, site, 1, slab, zs[near])
    g_two[pl.ds(site, 1), :] = partial
    wait_rows(3, grecv.at[1])
    whole = (g_two[0:1, :] + g_two[1:2, :]) + (g_two[2:3, :] + g_two[3:4, :])

    gram = [[None] * (HIST + 1) for i in range(HIST + 1)]
    for place, (i, j) in enumerate(order):
        value = jnp.sum(jnp.where(lane == place, whole, 0.0), axis=1, keepdims=True)
        gram[i][j] = gram[j][i] = jnp.broadcast_to(value, (1, 128))
    weights = [
        jnp.broadcast_to(jnp.concatenate([weight, weight], 1), (8, 256))
        for weight in solve_weights(gram)
    ]

    for a in range(SITES):

        def finish(c, carry):
            rows = pl.ds(pl.multiple_of(c * 8, 8), 8)
            offset = pl.ds(pl.multiple_of(a * ROWS + c * 8, 8), 8)
            value = weights[0] * ut[0, offset, :]
            for i in range(1, HIST):
                value = value + weights[i] * ut[i, offset, :]
            res[a, rows, :] = value + weights[HIST] * tv[a, rows, :]
            return carry

        lax.fori_loop(0, ROWS // 8, finish, 0, unroll=4)
        pltpu.make_async_copy(res.at[a], next_hbm.at[a], out_sem.at[SITES + a]).start()

    for q in range(SITES):
        arrived(fsend.at[q])
        arrived(bsend.at[q])
    wait_rows(31, gsend.at[0])
    wait_rows(3, gsend.at[1])
    for a in range(SITES):
        pltpu.make_async_copy(hv.at[a], last_hbm.at[a], out_sem.at[a]).wait()
        pltpu.make_async_copy(res.at[a], next_hbm.at[a], out_sem.at[SITES + a]).wait()


def step(potential, t_now, hist_t, hist_r, chi_self, chi_cross):
    flat = (SITES, ROWS, N)
    wz, cs, hh = tables()
    vm = pltpu.VMEM
    field = jax.ShapeDtypeStruct(flat, F32)
    scratch = [
        vm(flat, F32), vm(flat, F32),
        vm((HIST, SITES * ROWS, N), F32), vm((HIST, SITES * ROWS, N), F32),
        vm((6, N, N), F32), vm((6, N, N), F32),
        vm((256, 768), BF16), vm((768, 256), BF16), vm((512, 768), BF16),
        vm((512, 1536), BF16), vm((1536, 512), BF16),
        vm((SITES, 1024, 128), F32), vm((SITES, 4, 256, 128), F32),
        vm((SITES, 512, 256), F32), vm((SITES, 512, 256), F32),
        vm((SITES, 4, 256, 128), F32), vm((SITES, 1024, 128), F32),
        vm((512, 768), BF16), vm((256, 512), F32), vm((768, 512), BF16),
        vm((512, 512), F32), vm((256, 1536), BF16), vm((512, 768), BF16),
        vm((256, 1536), BF16), vm((512, 768), BF16), vm((512, 256), F32),
        vm((8, 128), F32), vm((32, 128), F32), vm((8, 128), F32), vm((8, 128), F32),
        vm(flat, F32),
        pltpu.SemaphoreType.DMA((40,)), pltpu.SemaphoreType.DMA((6,)),
        pltpu.SemaphoreType.DMA((3,)), pltpu.SemaphoreType.DMA((3,)),
        pltpu.SemaphoreType.DMA((3,)), pltpu.SemaphoreType.DMA((3,)),
        pltpu.SemaphoreType.DMA((2,)), pltpu.SemaphoreType.DMA((2,)),
    ]
    anywhere = pl.BlockSpec(memory_space=pl.ANY)
    t_next, residual = pl.pallas_call(
        kernel,
        out_shape=(field, field),
        in_specs=[anywhere] * 9,
        out_specs=(anywhere, anywhere),
        scratch_shapes=scratch,
        compiler_params=pltpu.CompilerParams(
            collective_id=0, has_side_effects=True, vmem_limit_bytes=56 * 1024 * 1024
        ),
    )(
        potential.reshape(flat),
        t_now.reshape(flat),
        hist_t.reshape(HIST, SITES * ROWS, N),
        hist_r.reshape(HIST, SITES * ROWS, N),
        chi_self,
        chi_cross,
        jnp.asarray(wz),
        jnp.asarray(cs),
        jnp.asarray(hh),
    )
    return t_next.reshape(t_now.shape), residual.reshape(t_now.shape)


def solution(mesh):
    field = P(None, "slab", "site", None)
    past = P(None, None, "slab", "site", None)
    chi = P(None, ("slab", "site"), None, None)
    return jax.shard_map(
        step,
        mesh=mesh,
        in_specs=(field, field, past, past, chi, chi),
        out_specs=(field, field),
        check_vma=False,
    )
```

profile of v0, /device:TPU:1, one launch (start us, length us, event | category | flops | bytes accessed | tf_op | source)
XLA Modules:
  0.0 72.6 jit_solution(10033689340514060769)
XLA Ops:
  0.6 68.0 %shard_map.104 = (f32[3,512,256]{2,1,0:T(8,128)}, f32[3,512,256]{2,1,0:T(8,128)}) custom-call(f32[3,512,256]{2,1,0:T(8,128)} %bitcast.8, f32[3,512,256]{2,1,0:T(8,128)} %bitcast.9, f32[4,1536,256]{2,1,0:T(8,128)} %bitcast.6, f32[4,1536,256]{2,1,0:T(8,128)} %bitcast.7, f32[3,2,256,256]{3,2,1,0:T(8,128)} %self_hbm.1, f32[3,2,256,256]{3,2,1,0:T(8,128)} %cross_hbm.1, ...), custom_call_target="tpu_custom_call" | custom-call | tf_op jit(solution)/shard_map/pallas_call | solution.py:483
  68.6 0.0 copy-start
  68.6 2.8 %copy.13 = f32[3,8,64,256]{3,2,1,0:T(8,128)} copy(f32[3,8,64,256]{3,2,1,0:T(8,128)} %bitcast.11) | data formatting | bytes 3145728
  71.4 0.0 copy-done
  71.4 1.1 %copy.14 = f32[3,8,64,256]{3,2,1,0:T(8,128)} copy(f32[3,8,64,256]{3,2,1,0:T(8,128)S(1)} %bitcast.10) | data formatting | bytes 3145728
Async XLA Ops:
  68.6 2.8 %copy-start = (f32[3,512,256]{2,1,0:T(8,128)S(1)}, f32[3,512,256]{2,1,0:T(8,128)}, u32[]{:S(2)}) copy-start(f32[3,512,256]{2,1,0:T(8,128)} %get-tuple-element.5) | copy-start | bytes 4718596
where the time goes:
time: 72.8 us; the launch traced here: 72.6 us
  Pallas kernels  68 us (93%)
  local copies, waits for them, and re-layouts  3.97 us (5%)
    pallas_call x1, Pallas kernels, step(): pl.pallas_call(kernel, out_shape=(field, field), in_specs=[anywhere] * 9,...  68 us
    unnamed x4, local copies, waits for them, and re-layouts  3.97 us

commit v1 on v0

--- a/solution.py
+++ b/solution.py
@@ -42,7 +42,10 @@
     blocks = np.stack([cosine.reshape(N, 4, 64), sine.reshape(N, 4, 64)], 2).reshape(N, 512)
     turned = np.stack([-sine.reshape(N, 4, 64), cosine.reshape(N, 4, 64)], 2).reshape(N, 512)
     along_y = np.concatenate([blocks, turned], 0)
-    return split_table(along_z), split_table(along_x), split_table(along_y)
+    waves = np.arange(HALF).reshape(16, 2, 4)
+    cuts = [split_table(along_z[np.concatenate([w, w + HALF])]) for w in (waves[:, c].ravel() for c in (0, 1))]
+    from_z = np.stack([np.concatenate([cut[0], cut[1], cut[0]], 0) for cut in cuts])
+    return split_table(along_z), split_table(along_x), split_table(along_y), from_z
 
 
 def halves(value):
@@ -86,14 +89,14 @@
 
 
 def kernel(
-    pot_hbm, t_hbm, hist_t_hbm, hist_r_hbm, self_hbm, cross_hbm, wz_hbm, cs_hbm, h_hbm,
-    next_hbm, last_hbm,
+    pot_hbm, t_hbm, hist_t_hbm, hist_r_hbm, self_hbm, cross_hbm, wz_hbm, cs_hbm, h_hbm, wb_hbm,
+    next_ref, last_ref,
     tv, hv, ut, hr, low_chi, top_chi,
-    wz_wide, wz_tall, cs_wide, h_wide, h_tall,
+    wz_wide, w_back, cs_wide, h_wide, h_tall,
     sent, got, spec, spec_top, back, home,
     d_b, z_f, r_b, zz_f, u_b, m_b, t_b, e_b, y_f,
-    g_row, g_one, g_mid, g_two, res,
-    in_sem, out_sem, fsend, frecv, bsend, brecv, gsend, grecv,
+    g_row, g_all,
+    in_sem, fsend, frecv, bsend, brecv, gsend, grecv,
 ):
     slab = lax.axis_index("slab")
     site = lax.axis_index("site")
@@ -126,36 +129,54 @@
     for a in range(SITES):
         load(("sl", a), self_hbm.at[a, 0], low_chi.at[a])
         load(("cl", a), cross_hbm.at[a, 0], low_chi.at[3 + a])
-        load(("st", a), self_hbm.at[a, 1], top_chi.at[a])
-        load(("ct", a), cross_hbm.at[a, 1], top_chi.at[3 + a])
     for part in range(3):
         load(("ht", part), h_hbm.at[part % 2], h_tall.at[pl.ds(512 * part, 512)])
-        load(("wt", part), wz_hbm.at[part % 2], wz_tall.at[pl.ds(256 * part, 256)])
+    load("wb", wb_hbm, w_back)
+    top_copies = []
+    for a in range(SITES):
+        for place, src in ((a, self_hbm), (3 + a, cross_hbm)):
+            top_copies.append(
+                pltpu.make_async_copy(src.at[a, 1], top_chi.at[place], in_sem.at[counter[0]])
+            )
+            counter[0] += 1
+
+    @pl.when(leading)
+    def _():
+        for copy in top_copies:
+            copy.start()
 
     cores = [core, (core + 1) % 2]
-    zs = [(site + step) % 4 for step in range(4)]
-
-    def chip(group):
-        return ((py + group // 4) % 4) * 4 + (px + group % 4) % 4
-
-    def over_peers(action):
-        base = chip(0) * 2
-        for near in range(1, 8):
-            action(base + cores[near // 4], zs[near % 4])
-
+    zs = [(site + step) % 4 for step in (2, 1, 3, 0)]
+
+    def distance(place):
+        return jnp.where(place < 2, 2 - place, (place + 1) % 4)
+
+    def over_peers(action, sides):
         def step(group, carry):
-            base = chip(group) * 2
-            for near in range(8):
-                action(base + cores[near // 4], zs[near % 4])
+            chip = ((py + distance(group // 4)) % 4) * 4 + (px + distance(group % 4)) % 4
+            for side in sides:
+                for z in zs:
+                    action(chip * 2 + side, z)
             return carry
 
-        lax.fori_loop(1, 16, step, 0)
+        lax.fori_loop(0, 15, step, 0)
+        for side in sides:
+            for z in zs[:3]:
+                action(plane * 2 + side, z)
+            if side is cores[1]:
+                action(plane * 2 + side, site)
+            elif side is not cores[0]:
+
+                @pl.when(core != side)
+                def _():
+                    action(plane * 2 + side, site)
 
     barrier = pltpu.get_barrier_semaphore()
     over_peers(
         lambda sl, st: pl.semaphore_signal(
             barrier, inc=1, device_id=(sl, st), device_id_type=MESH
-        )
+        ),
+        cores,
     )
 
     lane = lax.broadcasted_iota(jnp.int32, (1, 128), 1)
@@ -187,7 +208,7 @@
             sent[q, pl.ds(2 * pair, 128, stride=8), :] = first
             sent[q, pl.ds(2 * pair + 1, 128, stride=8), :] = second
 
-    def send_forward(q):
+    def send_forward(q, side):
         def action(sl, st):
             wave = pl.multiple_of((sl * 4 + st) * 8, 8)
             pltpu.make_async_remote_copy(
@@ -199,7 +220,9 @@
                 device_id_type=MESH,
             ).start()
 
-        over_peers(action)
+        over_peers(action, (side,))
+
+    def keep_own(q):
         got[q, site, pl.ds(pl.multiple_of(slab * 8, 8), 8), :] = sent[
             q, pl.ds(pl.multiple_of(me * 8, 8), 8), :
         ]
@@ -211,9 +234,6 @@
             for part in range(3):
                 copies[f"wz{part}"].wait()
         forward_site(q)
-        if q == 0:
-            pl.semaphore_wait(barrier, PEERS)
-        send_forward(q)
 
     copies["r"].wait()
     copies["u"].wait()
@@ -227,14 +247,37 @@
 
     zero = jnp.zeros((8, 256), F32)
     past = lax.fori_loop(0, SITES * ROWS // 8, history, (zero,) * len(PAIRS))
+
+    def pack(entries, first):
+        row = jnp.zeros((1, 128), F32)
+        for place, entry in enumerate(entries):
+            folded = entry[:, 0:128] + entry[:, 128:256]
+            value = jnp.sum(jnp.sum(folded, axis=0, keepdims=True), axis=1, keepdims=True)
+            row = jnp.where(lane == first + place, value, row)
+        return row
+
+    past_row = pack(past, 0)
+
+    pl.semaphore_wait(barrier, PEERS)
+    for side in range(2):
+        for q in range(SITES):
+            send_forward(q, side)
+    for q in range(SITES):
+        keep_own(q)
+
     for part in range(3):
         copies[("cs", part)].wait()
         copies[("hw", part)].wait()
         copies[("ht", part)].wait()
-        copies[("wt", part)].wait()
+    copies["wb"].wait()
     for a in range(SITES):
-        for kind in ("sl", "cl", "st", "ct"):
-            copies[(kind, a)].wait()
+        copies[("sl", a)].wait()
+        copies[("cl", a)].wait()
+
+    @pl.when(leading)
+    def _():
+        for copy in top_copies:
+            copy.wait()
 
     def arrived(sem):
         block = sent.at[0, pl.ds(0, PEERS * 8)]
@@ -296,6 +339,8 @@
         m_b[rows, 0:256] = high
         m_b[rows, 256:512] = high
         m_b[rows, 512:768] = low
+
+    shelf = pl.multiple_of((plane * 4 + site) * 8, 8)
 
     def back_site(a, carry):
         def mix(c, carry):
@@ -336,95 +381,105 @@
         def action(sl, st):
             pltpu.make_async_remote_copy(
                 src_ref=back.at[a, st, pl.ds(pl.multiple_of(sl * 8, 8), 8)],
-                dst_ref=home.at[a, pl.ds(pl.multiple_of(me * 8, 8), 8)],
+                dst_ref=home.at[a, core, pl.ds(shelf, 8)],
                 send_sem=bsend.at[a],
-                recv_sem=brecv.at[a],
+                recv_sem=brecv.at[core * 3 + a],
                 device_id=(sl, st),
                 device_id_type=MESH,
             ).start()
 
-        over_peers(action)
-        home[a, pl.ds(pl.multiple_of(me * 8, 8), 8), :] = back[
+        over_peers(action, cores)
+        home[a, core, pl.ds(shelf, 8), :] = back[
             a, site, pl.ds(pl.multiple_of(slab * 8, 8), 8), :
         ]
         return carry
 
     lax.fori_loop(0, SITES, back_site, 0)
 
-    def home_site(a, sums):
-        arrived(brecv.at[a])
-        for x in range(8):
-            lines = jnp.transpose(home[a, pl.ds(x, 128, stride=8), :])
-            high, low = halves(jnp.concatenate([lines[0:64], lines[64:128]], 1))
-            rows = pl.ds(64 * x, 64)
-            e_b[rows, 0:256] = high
-            e_b[rows, 256:512] = high
-            e_b[rows, 512:768] = low
-        y_f[...] = lax.dot_general(e_b[...], wz_tall[...], NN, preferred_element_type=F32)
+    def arrived_home(a, side):
+        @pl.when(core == side)
+        def _():
+            block = sent.at[0, pl.ds(0, 63 * 8)]
+            pltpu.make_async_copy(block, block, brecv.at[side * 3 + a]).wait()
+
+        @pl.when(core != side)
+        def _():
+            block = sent.at[0, pl.ds(0, 64 * 8)]
+            pltpu.make_async_copy(block, block, brecv.at[side * 3 + a]).wait()
+
+    def along_z(a, side):
+        arrived_home(a, side)
+        for pair in range(4):
+            lines = jnp.transpose(
+                jnp.concatenate(
+                    [home[a, side, pl.ds(2 * pair + x, 64, stride=8), :] for x in range(2)], 0
+                )
+            )
+            real, imag = lines[0:64], lines[64:128]
+            first = jnp.where(real_half, real, swap(imag))
+            second = jnp.where(real_half, swap(real), imag)
+            for x, value in ((2 * pair, first), (2 * pair + 1, second)):
+                high, low = halves(value)
+                rows = pl.ds(64 * x, 64)
+                e_b[rows, 0:128] = high
+                e_b[rows, 128:256] = high
+                e_b[rows, 256:384] = low
+        y_f[...] = lax.dot_general(e_b[...], w_back[side], NN, preferred_element_type=F32)
+
+    def home_first(a, carry):
+        along_z(a, 0)
+
+        def chunk(c, carry):
+            rows = pl.ds(pl.multiple_of(c * 32, 32), 32)
+            hv[a, rows, :] = y_f[rows, :] - hv[a, rows, :]
+            return carry
+
+        return lax.fori_loop(0, ROWS // 32, chunk, carry)
+
+    lax.fori_loop(0, SITES, home_first, 0)
+
+    def home_second(a, sums):
+        along_z(a, 1)
 
         def chunk(c, sums):
             rows = pl.ds(pl.multiple_of(c * 8, 8), 8)
-            latest = y_f[rows, :] - hv[a, rows, :]
-            hv[a, rows, :] = latest
+            latest = y_f[rows, :] + hv[a, rows, :]
+            last_ref[a, rows, :] = latest
             tv[a, rows, :] = tv[a, rows, :] + MIXING * latest
             offset = pl.ds(pl.multiple_of(a * ROWS + c * 8, 8), 8)
             new = [s + hr[i, offset, :] * latest for i, s in enumerate(sums[:HIST])]
             return tuple(new) + (sums[HIST] + latest * latest,)
 
-        sums = lax.fori_loop(0, ROWS // 8, chunk, sums)
-        pltpu.make_async_copy(hv.at[a], last_hbm.at[a], out_sem.at[a]).start()
-        return sums
-
-    newest = lax.fori_loop(0, SITES, home_site, (zero,) * (HIST + 1))
-
-    entries = {pair: s for pair, s in zip(PAIRS, past)}
-    for i in range(HIST + 1):
-        entries[(i, HIST)] = newest[i]
-    order = sorted(entries)
-    row = jnp.zeros((1, 128), F32)
-    for place, pair in enumerate(order):
-        folded = entries[pair][:, 0:128] + entries[pair][:, 128:256]
-        value = jnp.sum(jnp.sum(folded, axis=0, keepdims=True), axis=1, keepdims=True)
-        row = jnp.where(lane == place, value, row)
+        return lax.fori_loop(0, ROWS // 8, chunk, sums, unroll=2)
+
+    newest = lax.fori_loop(0, SITES, home_second, (zero,) * (HIST + 1))
+
+    row = past_row + pack(newest, len(PAIRS))
     g_row[0:1, :] = row
 
-    def send_row(src, dst, slot, stage, sl, st):
+    def send_row(sl, st):
         pltpu.make_async_remote_copy(
-            src_ref=src.at[pl.ds(0, 1)],
-            dst_ref=dst.at[pl.ds(slot, 1)],
-            send_sem=gsend.at[stage],
-            recv_sem=grecv.at[stage],
+            src_ref=g_row.at[pl.ds(0, 1)],
+            dst_ref=g_all.at[pl.ds(me, 1)],
+            send_sem=gsend,
+            recv_sem=grecv,
             device_id=(sl, st),
             device_id_type=MESH,
         ).start()
 
-    for near in range(1, 2):
-        send_row(g_row, g_one, slab, 0, chip(0) * 2 + cores[near], site)
-
-    def spread(group, carry):
-        for near in range(2):
-            send_row(g_row, g_one, slab, 0, chip(group) * 2 + cores[near], site)
-        return carry
-
-    lax.fori_loop(1, 16, spread, 0)
-    g_one[pl.ds(slab, 1), :] = row
-
-    def wait_rows(count, sem):
-        block = g_one.at[pl.ds(0, count)]
+    over_peers(send_row, cores)
+    g_all[pl.ds(me, 1), :] = row
+
+    def wait_rows(sem):
+        block = g_all.at[pl.ds(0, PEERS)]
         pltpu.make_async_copy(block, block, sem).wait()
 
-    wait_rows(31, grecv.at[0])
-    partial = jnp.sum(g_one[...], axis=0, keepdims=True)
-    g_mid[0:1, :] = partial
-    for near in range(1, 4):
-        send_row(g_mid, g_two, site, 1, slab, zs[near])
-    g_two[pl.ds(site, 1), :] = partial
-    wait_rows(3, grecv.at[1])
-    whole = (g_two[0:1, :] + g_two[1:2, :]) + (g_two[2:3, :] + g_two[3:4, :])
+    wait_rows(grecv)
+    whole = jnp.sum(g_all[...], axis=0, keepdims=True)
 
     gram = [[None] * (HIST + 1) for i in range(HIST + 1)]
-    for place, (i, j) in enumerate(order):
-        value = jnp.sum(jnp.where(lane == place, whole, 0.0), axis=1, keepdims=True)
+    for index, (i, j) in enumerate(PAIRS + [(i, HIST) for i in range(HIST + 1)]):
+        value = jnp.sum(jnp.where(lane == index, whole, 0.0), axis=1, keepdims=True)
         gram[i][j] = gram[j][i] = jnp.broadcast_to(value, (1, 128))
     weights = [
         jnp.broadcast_to(jnp.concatenate([weight, weight], 1), (8, 256))
@@ -439,55 +494,49 @@
             value = weights[0] * ut[0, offset, :]
             for i in range(1, HIST):
                 value = value + weights[i] * ut[i, offset, :]
-            res[a, rows, :] = value + weights[HIST] * tv[a, rows, :]
+            next_ref[a, rows, :] = value + weights[HIST] * tv[a, rows, :]
             return carry
 
         lax.fori_loop(0, ROWS // 8, finish, 0, unroll=4)
-        pltpu.make_async_copy(res.at[a], next_hbm.at[a], out_sem.at[SITES + a]).start()
 
     for q in range(SITES):
         arrived(fsend.at[q])
         arrived(bsend.at[q])
-    wait_rows(31, gsend.at[0])
-    wait_rows(3, gsend.at[1])
-    for a in range(SITES):
-        pltpu.make_async_copy(hv.at[a], last_hbm.at[a], out_sem.at[a]).wait()
-        pltpu.make_async_copy(res.at[a], next_hbm.at[a], out_sem.at[SITES + a]).wait()
+    wait_rows(gsend)
 
 
 def step(potential, t_now, hist_t, hist_r, chi_self, chi_cross):
     flat = (SITES, ROWS, N)
-    wz, cs, hh = tables()
+    wz, cs, hh, wb = tables()
     vm = pltpu.VMEM
-    field = jax.ShapeDtypeStruct(flat, F32)
+    field = pltpu.VMEM(flat, F32)
     scratch = [
         vm(flat, F32), vm(flat, F32),
         vm((HIST, SITES * ROWS, N), F32), vm((HIST, SITES * ROWS, N), F32),
         vm((6, N, N), F32), vm((6, N, N), F32),
-        vm((256, 768), BF16), vm((768, 256), BF16), vm((512, 768), BF16),
+        vm((256, 768), BF16), vm((2, 384, 256), BF16), vm((512, 768), BF16),
         vm((512, 1536), BF16), vm((1536, 512), BF16),
         vm((SITES, 1024, 128), F32), vm((SITES, 4, 256, 128), F32),
         vm((SITES, 512, 256), F32), vm((SITES, 512, 256), F32),
-        vm((SITES, 4, 256, 128), F32), vm((SITES, 1024, 128), F32),
+        vm((SITES, 4, 256, 128), F32), vm((SITES, 2, 512, 128), F32),
         vm((512, 768), BF16), vm((256, 512), F32), vm((768, 512), BF16),
         vm((512, 512), F32), vm((256, 1536), BF16), vm((512, 768), BF16),
-        vm((256, 1536), BF16), vm((512, 768), BF16), vm((512, 256), F32),
-        vm((8, 128), F32), vm((32, 128), F32), vm((8, 128), F32), vm((8, 128), F32),
-        vm(flat, F32),
-        pltpu.SemaphoreType.DMA((40,)), pltpu.SemaphoreType.DMA((6,)),
+        vm((256, 1536), BF16), vm((512, 384), BF16), vm((512, 256), F32),
+        vm((8, 128), F32), vm((128, 128), F32),
+        pltpu.SemaphoreType.DMA((40,)),
         pltpu.SemaphoreType.DMA((3,)), pltpu.SemaphoreType.DMA((3,)),
-        pltpu.SemaphoreType.DMA((3,)), pltpu.SemaphoreType.DMA((3,)),
-        pltpu.SemaphoreType.DMA((2,)), pltpu.SemaphoreType.DMA((2,)),
+        pltpu.SemaphoreType.DMA((3,)), pltpu.SemaphoreType.DMA((6,)),
+        pltpu.SemaphoreType.DMA, pltpu.SemaphoreType.DMA,
     ]
-    anywhere = pl.BlockSpec(memory_space=pl.ANY)
+    anywhere = pl.BlockSpec(memory_space=pltpu.HBM)
     t_next, residual = pl.pallas_call(
         kernel,
         out_shape=(field, field),
-        in_specs=[anywhere] * 9,
-        out_specs=(anywhere, anywhere),
+        in_specs=[anywhere] * 10,
+        out_specs=(pl.BlockSpec(memory_space=pltpu.VMEM),) * 2,
         scratch_shapes=scratch,
         compiler_params=pltpu.CompilerParams(
-            collective_id=0, has_side_effects=True, vmem_limit_bytes=56 * 1024 * 1024
+            collective_id=0, has_side_effects=True, vmem_limit_bytes=60 * 1024 * 1024 + 512 * 1024
         ),
     )(
         potential.reshape(flat),
@@ -499,6 +548,7 @@
         jnp.asarray(wz),
         jnp.asarray(cs),
         jnp.asarray(hh),
+        jnp.asarray(wb),
     )
     return t_next.reshape(t_now.shape), residual.reshape(t_now.shape)
 

time: 72.8 us -> 64.5 us (0.89)
  Pallas kernels: 68 us -> 61.5 us
  local copies, waits for them, and re-layouts: 3.97 us -> 2.29 us
    pallas_call x1, Pallas kernels: 68 us -> 61.5 us  [step(): pl.pallas_call(kernel, out_shape=(field, field), in_specs=[anywhere] * 10...]
    unnamed x4 -> x2, local copies, waits for them, and re-layouts: 3.97 us -> 2.29 us
where the time goes in v1:
time: 64.5 us; the launch traced here: 64.4 us
  Pallas kernels  61.5 us (95%)
  local copies, waits for them, and re-layouts  2.29 us (4%)
    pallas_call x1, Pallas kernels, step(): pl.pallas_call(kernel, out_shape=(field, field), in_specs=[anywhere] * 10...  61.5 us
    unnamed x2, local copies, waits for them, and re-layouts  2.29 us

profile of v1, /device:TPU:1, one launch (start us, length us, event | category | flops | bytes accessed | tf_op | source)
XLA Modules:
  0.0 64.4 jit_solution(3625757766748789113)
XLA Ops:
  0.6 61.5 %shard_map.113 = (f32[3,512,256]{2,1,0:T(8,128)S(1)}, f32[3,512,256]{2,1,0:T(8,128)S(1)}) custom-call(f32[3,512,256]{2,1,0:T(8,128)} %bitcast.10, f32[3,512,256]{2,1,0:T(8,128)} %bitcast.11, f32[4,1536,256]{2,1,0:T(8,128)} %bitcast.8, f32[4,1536,256]{2,1,0:T(8,128)} %bitcast.9, f32[3,2,256,256]{3,2,1,0:T(8,128)} %self_hbm.1, f32[3,2,256,256]{3,2,1,0:T(8,128)} %cross_hbm.1, ...), custom_call_target="tpu_custom_call" | custom-call | tf_op jit(solution)/shard_map/pallas_call | solution.py:532
  62.1 1.1 %copy.14 = f32[3,8,64,256]{3,2,1,0:T(8,128)} copy(f32[3,8,64,256]{3,2,1,0:T(8,128)S(1)} %bitcast.7) | data formatting | bytes 3145728
  63.2 1.1 %copy.15 = f32[3,8,64,256]{3,2,1,0:T(8,128)} copy(f32[3,8,64,256]{3,2,1,0:T(8,128)S(1)} %bitcast.6) | data formatting | bytes 3145728

commit v2 on v1

--- a/solution.py
+++ b/solution.py
@@ -90,8 +90,8 @@
 
 def kernel(
     pot_hbm, t_hbm, hist_t_hbm, hist_r_hbm, self_hbm, cross_hbm, wz_hbm, cs_hbm, h_hbm, wb_hbm,
-    next_ref, last_ref,
-    tv, hv, ut, hr, low_chi, top_chi,
+    weight_ref, ut, tv, last_ref,
+    hv, hr, low_chi, top_chi,
     wz_wide, w_back, cs_wide, h_wide, h_tall,
     sent, got, spec, spec_top, back, home,
     d_b, z_f, r_b, zz_f, u_b, m_b, t_b, e_b, y_f,
@@ -121,30 +121,6 @@
             load("wz0", wz_hbm.at[0], wz_wide.at[:, pl.ds(0, 256)])
             load("wz1", wz_hbm.at[1], wz_wide.at[:, pl.ds(256, 256)])
             load("wz2", wz_hbm.at[0], wz_wide.at[:, pl.ds(512, 256)])
-    load("r", hist_r_hbm, hr)
-    load("u", hist_t_hbm, ut)
-    for part in range(3):
-        load(("cs", part), cs_hbm.at[part % 2], cs_wide.at[:, pl.ds(256 * part, 256)])
-        load(("hw", part), h_hbm.at[part % 2], h_wide.at[:, pl.ds(512 * part, 512)])
-    for a in range(SITES):
-        load(("sl", a), self_hbm.at[a, 0], low_chi.at[a])
-        load(("cl", a), cross_hbm.at[a, 0], low_chi.at[3 + a])
-    for part in range(3):
-        load(("ht", part), h_hbm.at[part % 2], h_tall.at[pl.ds(512 * part, 512)])
-    load("wb", wb_hbm, w_back)
-    top_copies = []
-    for a in range(SITES):
-        for place, src in ((a, self_hbm), (3 + a, cross_hbm)):
-            top_copies.append(
-                pltpu.make_async_copy(src.at[a, 1], top_chi.at[place], in_sem.at[counter[0]])
-            )
-            counter[0] += 1
-
-    @pl.when(leading)
-    def _():
-        for copy in top_copies:
-            copy.start()
-
     cores = [core, (core + 1) % 2]
     zs = [(site + step) % 4 for step in (2, 1, 3, 0)]
 
@@ -233,7 +209,37 @@
         if q == 0:
             for part in range(3):
                 copies[f"wz{part}"].wait()
+            load("r", hist_r_hbm, hr)
+            load("u", hist_t_hbm, ut)
+            for part in range(3):
+                load(("cs", part), cs_hbm.at[part % 2], cs_wide.at[:, pl.ds(256 * part, 256)])
+                load(("hw", part), h_hbm.at[part % 2], h_wide.at[:, pl.ds(512 * part, 512)])
+            for a in range(SITES):
+                load(("sl", a), self_hbm.at[a, 0], low_chi.at[a])
+                load(("cl", a), cross_hbm.at[a, 0], low_chi.at[3 + a])
+            for part in range(3):
+                load(("ht", part), h_hbm.at[part % 2], h_tall.at[pl.ds(512 * part, 512)])
+            load("wb", wb_hbm, w_back)
+            top_copies = []
+            for a in range(SITES):
+                for place, src in ((a, self_hbm), (3 + a, cross_hbm)):
+                    top_copies.append(
+                        pltpu.make_async_copy(src.at[a, 1], top_chi.at[place], in_sem.at[counter[0]])
+                    )
+                    counter[0] += 1
+
+            @pl.when(leading)
+            def _():
+                for copy in top_copies:
+                    copy.start()
+
         forward_site(q)
+        if q == 0:
+            pl.semaphore_wait(barrier, PEERS)
+        send_forward(q, 0)
+    for q in range(SITES):
+        send_forward(q, 1)
+        keep_own(q)
 
     copies["r"].wait()
     copies["u"].wait()
@@ -257,13 +263,6 @@
         return row
 
     past_row = pack(past, 0)
-
-    pl.semaphore_wait(barrier, PEERS)
-    for side in range(2):
-        for q in range(SITES):
-            send_forward(q, side)
-    for q in range(SITES):
-        keep_own(q)
 
     for part in range(3):
         copies[("cs", part)].wait()
@@ -481,11 +480,21 @@
     for index, (i, j) in enumerate(PAIRS + [(i, HIST) for i in range(HIST + 1)]):
         value = jnp.sum(jnp.where(lane == index, whole, 0.0), axis=1, keepdims=True)
         gram[i][j] = gram[j][i] = jnp.broadcast_to(value, (1, 128))
-    weights = [
-        jnp.broadcast_to(jnp.concatenate([weight, weight], 1), (8, 256))
-        for weight in solve_weights(gram)
-    ]
-
+    for i, weight in enumerate(solve_weights(gram)):
+        weight_ref[i : i + 1, :] = weight
+
+    for q in range(SITES):
+        arrived(fsend.at[q])
+        arrived(bsend.at[q])
+    wait_rows(gsend)
+
+
+def last_kernel(weight_ref, ut, tv, last_vmem, next_hbm, last_hbm, res, sem):
+    pltpu.make_async_copy(last_vmem, last_hbm, sem.at[SITES]).start()
+    weights = []
+    for i in range(HIST + 1):
+        weight = weight_ref[i : i + 1, :]
+        weights.append(jnp.broadcast_to(jnp.concatenate([weight, weight], 1), (8, 256)))
     for a in range(SITES):
 
         def finish(c, carry):
@@ -494,15 +503,14 @@
             value = weights[0] * ut[0, offset, :]
             for i in range(1, HIST):
                 value = value + weights[i] * ut[i, offset, :]
-            next_ref[a, rows, :] = value + weights[HIST] * tv[a, rows, :]
+            res[a, rows, :] = value + weights[HIST] * tv[a, rows, :]
             return carry
 
         lax.fori_loop(0, ROWS // 8, finish, 0, unroll=4)
-
-    for q in range(SITES):
-        arrived(fsend.at[q])
-        arrived(bsend.at[q])
-    wait_rows(gsend)
+        pltpu.make_async_copy(res.at[a], next_hbm.at[a], sem.at[a]).start()
+    for a in range(SITES):
+        pltpu.make_async_copy(res.at[a], next_hbm.at[a], sem.at[a]).wait()
+    pltpu.make_async_copy(last_vmem, last_hbm, sem.at[SITES]).wait()
 
 
 def step(potential, t_now, hist_t, hist_r, chi_self, chi_cross):
@@ -510,9 +518,9 @@
     wz, cs, hh, wb = tables()
     vm = pltpu.VMEM
     field = pltpu.VMEM(flat, F32)
+    whole = pl.BlockSpec(memory_space=pltpu.VMEM)
     scratch = [
-        vm(flat, F32), vm(flat, F32),
-        vm((HIST, SITES * ROWS, N), F32), vm((HIST, SITES * ROWS, N), F32),
+        vm(flat, F32), vm((HIST, SITES * ROWS, N), F32),
         vm((6, N, N), F32), vm((6, N, N), F32),
         vm((256, 768), BF16), vm((2, 384, 256), BF16), vm((512, 768), BF16),
         vm((512, 1536), BF16), vm((1536, 512), BF16),
@@ -529,14 +537,14 @@
         pltpu.SemaphoreType.DMA, pltpu.SemaphoreType.DMA,
     ]
     anywhere = pl.BlockSpec(memory_space=pltpu.HBM)
-    t_next, residual = pl.pallas_call(
+    inner = pl.pallas_call(
         kernel,
-        out_shape=(field, field),
+        out_shape=(vm((8, 128), F32), vm((HIST, SITES * ROWS, N), F32), field, field),
         in_specs=[anywhere] * 10,
-        out_specs=(pl.BlockSpec(memory_space=pltpu.VMEM),) * 2,
+        out_specs=(whole,) * 4,
         scratch_shapes=scratch,
         compiler_params=pltpu.CompilerParams(
-            collective_id=0, has_side_effects=True, vmem_limit_bytes=60 * 1024 * 1024 + 512 * 1024
+            collective_id=0, has_side_effects=True, vmem_limit_bytes=54 * 1024 * 1024
         ),
     )(
         potential.reshape(flat),
@@ -550,6 +558,15 @@
         jnp.asarray(hh),
         jnp.asarray(wb),
     )
+    outer = jax.ShapeDtypeStruct(flat, F32)
+    t_next, residual = pl.pallas_call(
+        last_kernel,
+        out_shape=(outer, outer),
+        in_specs=[whole] * 4,
+        out_specs=(anywhere, anywhere),
+        scratch_shapes=[vm(flat, F32), pltpu.SemaphoreType.DMA((SITES + 1,))],
+        compiler_params=pltpu.CompilerParams(vmem_limit_bytes=16 * 1024 * 1024),
+    )(*inner)
     return t_next.reshape(t_now.shape), residual.reshape(t_now.shape)
 
 

time: 64.5 us -> 59 us (0.915)
  Pallas kernels: 61.5 us -> 58.2 us
  local copies, waits for them, and re-layouts: 2.29 us -> 0 us
    pallas_call x1 -> x2, Pallas kernels: 61.5 us -> 58.2 us  [the longest x1 56.5 us: step(): pl.pallas_call(kernel, out_shape=(vm((8, 128), F32), vm((HIST, SITES * RO...]
    unnamed x2 -> x0, local copies, waits for them, and re-layouts: 2.29 us -> none
where the time goes in v2:
time: 59 us; the launch traced here: 58.9 us
  Pallas kernels  58.2 us (99%)
  between operations  0.64 us (1%)
    pallas_call x1, Pallas kernels, step(): pl.pallas_call(kernel, out_shape=(vm((8, 128), F32), vm((HIST, SITES * RO...  56.5 us
    pallas_call x1, Pallas kernels, step(): pl.pallas_call(last_kernel, out_shape=(outer, outer), in_specs=[whole] *...  1.69 us

profile of v2, /device:TPU:1, one launch (start us, length us, event | category | flops | bytes accessed | tf_op | source)
XLA Modules:
  0.0 58.9 jit_solution(4115819365156984777)
XLA Ops:
  0.6 56.5 %shard_map.113 = (f32[8,128]{1,0:T(8,128)S(1)}, f32[4,1536,256]{2,1,0:T(8,128)S(1)}, f32[3,512,256]{2,1,0:T(8,128)S(1)}, f32[3,512,256]{2,1,0:T(8,128)S(1)}) custom-call(f32[3,512,256]{2,1,0:T(8,128)} %bitcast.8, f32[3,512,256]{2,1,0:T(8,128)} %bitcast.9, f32[4,1536,256]{2,1,0:T(8,128)} %bitcast.6, f32[4,1536,256]{2,1,0:T(8,128)} %bitcast.7, ...), custom_call_target="tpu_custom_call" | custom-call | tf_op jit(solution)/shard_map/pallas_call | solution.py:540
  57.2 1.7 %shard_map.114 = (f32[3,512,256]{2,1,0:T(8,128)}, f32[3,512,256]{2,1,0:T(8,128)}) custom-call(f32[8,128]{1,0:T(8,128)S(1)} %get-tuple-element.8.weight_ref, f32[4,1536,256]{2,1,0:T(8,128)S(1)} %get-tuple-element.9.ut, f32[3,512,256]{2,1,0:T(8,128)S(1)} %get-tuple-element.10.tv, f32[3,512,256]{2,1,0:T(8,128)S(1)} %get-tuple-element.11.last_vmem), custom_call_target="tpu_custom_call" | custom-call | tf_op jit(solution)/shard_map/pallas_call | solution.py:562

commit v3 on v2

--- a/solution.py
+++ b/solution.py
@@ -236,9 +236,9 @@
         forward_site(q)
         if q == 0:
             pl.semaphore_wait(barrier, PEERS)
+        send_forward(q, 1)
+    for q in range(SITES):
         send_forward(q, 0)
-    for q in range(SITES):
-        send_forward(q, 1)
         keep_own(q)
 
     copies["r"].wait()
@@ -426,7 +426,7 @@
         y_f[...] = lax.dot_general(e_b[...], w_back[side], NN, preferred_element_type=F32)
 
     def home_first(a, carry):
-        along_z(a, 0)
+        along_z(a, 1)
 
         def chunk(c, carry):
             rows = pl.ds(pl.multiple_of(c * 32, 32), 32)
@@ -438,7 +438,7 @@
     lax.fori_loop(0, SITES, home_first, 0)
 
     def home_second(a, sums):
-        along_z(a, 1)
+        along_z(a, 0)
 
         def chunk(c, sums):
             rows = pl.ds(pl.multiple_of(c * 8, 8), 8)
@@ -449,7 +449,7 @@
             new = [s + hr[i, offset, :] * latest for i, s in enumerate(sums[:HIST])]
             return tuple(new) + (sums[HIST] + latest * latest,)
 
-        return lax.fori_loop(0, ROWS // 8, chunk, sums, unroll=2)
+        return lax.fori_loop(0, ROWS // 8, chunk, sums, unroll=8)
 
     newest = lax.fori_loop(0, SITES, home_second, (zero,) * (HIST + 1))
 

time: 59 us -> 57.9 us (0.981)
  Pallas kernels: 58.2 us -> 57.2 us
    pallas_call x1, Pallas kernels: 56.5 us -> 55.5 us  [step(): pl.pallas_call(kernel, out_shape=(vm((8, 128), F32), vm((HIST, SITES * RO...]
where the time goes in v3:
time: 57.9 us; the launch traced here: 57.8 us
  Pallas kernels  57.2 us (99%)
  between operations  0.64 us (1%)
    pallas_call x1, Pallas kernels, step(): pl.pallas_call(kernel, out_shape=(vm((8, 128), F32), vm((HIST, SITES * RO...  55.5 us
    pallas_call x1, Pallas kernels, step(): pl.pallas_call(last_kernel, out_shape=(outer, outer), in_specs=[whole] *...  1.69 us

profile of v3, /device:TPU:1, one launch (start us, length us, event | category | flops | bytes accessed | tf_op | source)
XLA Modules:
  0.0 57.8 jit_solution(9377807435703255491)
XLA Ops:
  0.6 55.5 %shard_map.113 = (f32[8,128]{1,0:T(8,128)S(1)}, f32[4,1536,256]{2,1,0:T(8,128)S(1)}, f32[3,512,256]{2,1,0:T(8,128)S(1)}, f32[3,512,256]{2,1,0:T(8,128)S(1)}) custom-call(f32[3,512,256]{2,1,0:T(8,128)} %bitcast.8, f32[3,512,256]{2,1,0:T(8,128)} %bitcast.9, f32[4,1536,256]{2,1,0:T(8,128)} %bitcast.6, f32[4,1536,256]{2,1,0:T(8,128)} %bitcast.7, ...), custom_call_target="tpu_custom_call" | custom-call | tf_op jit(solution)/shard_map/pallas_call | solution.py:540
  56.1 1.7 %shard_map.114 = (f32[3,512,256]{2,1,0:T(8,128)}, f32[3,512,256]{2,1,0:T(8,128)}) custom-call(f32[8,128]{1,0:T(8,128)S(1)} %get-tuple-element.8.weight_ref, f32[4,1536,256]{2,1,0:T(8,128)S(1)} %get-tuple-element.9.ut, f32[3,512,256]{2,1,0:T(8,128)S(1)} %get-tuple-element.10.tv, f32[3,512,256]{2,1,0:T(8,128)S(1)} %get-tuple-element.11.last_vmem), custom_call_target="tpu_custom_call" | custom-call | tf_op jit(solution)/shard_map/pallas_call | solution.py:562

commit v4 on v3

--- a/solution.py
+++ b/solution.py
@@ -56,29 +56,31 @@
 
 def solve_weights(gram):
     count = HIST + 1
+    inverse = []
     factor = [[None] * count for member in range(count)]
     for column in range(count):
         diagonal_sum = gram[column][column]
         for inner in range(column):
             diagonal_sum = diagonal_sum - factor[column][inner] * factor[column][inner]
         factor[column][column] = jnp.sqrt(diagonal_sum)
+        inverse.append(1.0 / factor[column][column])
         for row in range(column + 1, count):
             entry = gram[row][column]
             for inner in range(column):
                 entry = entry - factor[row][inner] * factor[column][inner]
-            factor[row][column] = entry / factor[column][column]
+            factor[row][column] = entry * inverse[column]
     middle = []
     for row in range(count):
         entry = jnp.ones_like(gram[0][0])
         for inner in range(row):
             entry = entry - factor[row][inner] * middle[inner]
-        middle.append(entry / factor[row][row])
+        middle.append(entry * inverse[row])
     weights = [None] * count
     for row in range(count - 1, -1, -1):
         entry = middle[row]
         for inner in range(row + 1, count):
             entry = entry - factor[inner][row] * weights[inner]
-        weights[row] = entry / factor[row][row]
+        weights[row] = entry * inverse[row]
     total = weights[0]
     for row in range(1, count):
         total = total + weights[row]
@@ -423,7 +425,11 @@
                 e_b[rows, 0:128] = high
                 e_b[rows, 128:256] = high
                 e_b[rows, 256:384] = low
-        y_f[...] = lax.dot_general(e_b[...], w_back[side], NN, preferred_element_type=F32)
+            if pair % 2:
+                part = pl.ds(128 * (pair - 1), 256)
+                y_f[part, :] = lax.dot_general(
+                    e_b[part, :], w_back[side], NN, preferred_element_type=F32
+                )
 
     def home_first(a, carry):
         along_z(a, 1)
@@ -506,7 +512,7 @@
             res[a, rows, :] = value + weights[HIST] * tv[a, rows, :]
             return carry
 
-        lax.fori_loop(0, ROWS // 8, finish, 0, unroll=4)
+        lax.fori_loop(0, ROWS // 8, finish, 0, unroll=8)
         pltpu.make_async_copy(res.at[a], next_hbm.at[a], sem.at[a]).start()
     for a in range(SITES):
         pltpu.make_async_copy(res.at[a], next_hbm.at[a], sem.at[a]).wait()

time: 57.9 us -> 57.8 us (level)
  no operation moved by 1% of the time
where the time goes in v4:
time: 57.8 us; the launch traced here: 57.7 us
  Pallas kernels  57 us (99%)
  between operations  0.64 us (1%)
    pallas_call x1, Pallas kernels, step(): pl.pallas_call(kernel, out_shape=(vm((8, 128), F32), vm((HIST, SITES * RO...  55.3 us
    pallas_call x1, Pallas kernels, step(): pl.pallas_call(last_kernel, out_shape=(outer, outer), in_specs=[whole] *...  1.69 us

profile of v4, /device:TPU:1, one launch (start us, length us, event | category | flops | bytes accessed | tf_op | source)
XLA Modules:
  0.0 57.7 jit_solution(10989298713738854272)
XLA Ops:
  0.6 55.3 %shard_map.113 = (f32[8,128]{1,0:T(8,128)S(1)}, f32[4,1536,256]{2,1,0:T(8,128)S(1)}, f32[3,512,256]{2,1,0:T(8,128)S(1)}, f32[3,512,256]{2,1,0:T(8,128)S(1)}) custom-call(f32[3,512,256]{2,1,0:T(8,128)} %bitcast.8, f32[3,512,256]{2,1,0:T(8,128)} %bitcast.9, f32[4,1536,256]{2,1,0:T(8,128)} %bitcast.6, f32[4,1536,256]{2,1,0:T(8,128)} %bitcast.7, ...), custom_call_target="tpu_custom_call" | custom-call | tf_op jit(solution)/shard_map/pallas_call | solution.py:546
  56.0 1.7 %shard_map.114 = (f32[3,512,256]{2,1,0:T(8,128)}, f32[3,512,256]{2,1,0:T(8,128)}) custom-call(f32[8,128]{1,0:T(8,128)S(1)} %get-tuple-element.8.weight_ref, f32[4,1536,256]{2,1,0:T(8,128)S(1)} %get-tuple-element.9.ut, f32[3,512,256]{2,1,0:T(8,128)S(1)} %get-tuple-element.10.tv, f32[3,512,256]{2,1,0:T(8,128)S(1)} %get-tuple-element.11.last_vmem), custom_call_target="tpu_custom_call" | custom-call | tf_op jit(solution)/shard_map/pallas_call | solution.py:568
